TPU v7x, 128 devices: a whole 4x4x4 slice. The times are simulated.
128 devices in a mesh: fsdp: 8 (over z_lo, x), tp: 16 (over y, z_hi, core).
Axes of the slice: x: 4, y: 4, z: 4 (z_hi: 2, z_lo: 2; z = z_hi * 2 + z_lo), core: 2. Of those that a mesh axis runs over, the one named last changes fastest.
Arguments:
- ref_gate: bfloat16 [6144, 11008], P('fsdp', 'tp'), may hold values from -6 to 6
- ref_up: bfloat16 [6144, 11008], P('fsdp', 'tp'), may hold values from -6 to 6
- ref_residual: bfloat16 [6144, 4096], P('fsdp', 'tp'), may hold values from -6 to 6
- ref_modality: int32 [6144], P('fsdp'), may hold values 0 or 1
- ref_down_text: bfloat16 [4096, 11008], P('fsdp', 'tp'), may hold values from -0.0546875 to 0.0546875
- ref_down_image: bfloat16 [4096, 11008], P('fsdp', 'tp'), may hold values from -0.0546875 to 0.0546875
- pol_gate: bfloat16 [6144, 11008], P('fsdp', 'tp'), may hold values from -6 to 6
- pol_up: bfloat16 [6144, 11008], P('fsdp', 'tp'), may hold values from -6 to 6
- pol_modality: int32 [6144], P('fsdp'), may hold values 0 or 1
- pol_segment: int32 [6144], P('fsdp'), may hold values from 0 to 11, never falling along the last dimension, each value on 1 to 768 neighbouring positions
- pair_margin: float32 [6], replicated, may hold values from -30 to 30
- token_cotangent: bfloat16 [6144, 4096], P('fsdp', 'tp'), may hold values from -24 to 24
- pol_down_text: bfloat16 [4096, 11008], P('fsdp', 'tp'), may hold values from -0.0546875 to 0.0546875
- pol_down_image: bfloat16 [4096, 11008], P('fsdp', 'tp'), may hold values from -0.0546875 to 0.0546875
Outputs:
- ref_out: bfloat16 [6144, 4096], P('fsdp', 'tp')
- grad_gate: bfloat16 [6144, 11008], P('fsdp', 'tp')
- grad_up: bfloat16 [6144, 11008], P('fsdp', 'tp')
- grad_down_text: float32 [4096, 11008], P('fsdp', 'tp')
- grad_down_image: float32 [4096, 11008], P('fsdp', 'tp')
Inputs may be any that keep to these rules, and one draw needn't show every extreme that they name: `ref_modality`: 0 marks a text token, 1 an image token. `pol_modality`: 0 marks a text token, 1 an image token. `pol_segment`: response numbers never fall along the tokens; responses 2p and 2p + 1 are the chosen and the rejected response of pair p; every response has at least one token.
All inputs are finite; a program needn't handle non-finite values. No bound on the sum of `ref_modality` or of `pol_modality` on one device may be relied on, other than what follows from the above.
Results may differ from a plain program's by a relative error of at most 0.015.
Values may be sent and summed in bfloat16 or wider, within the bound.
No kernel may reach another device: no remote copies, remote signals or barrier semaphores. Data moves between devices by JAX's collectives and lax.ppermute only.
A program may use at most 128 MiB of HBM per device.

v0:
```python
import jax
import jax.numpy as jnp
from jax import lax
from jax.sharding import PartitionSpec as P

dpo_beta = 0.1


def sent_together(arrays, axis, dim, along):
    ends, at = ([], 0)
    for a in arrays[:-1]:
        at += a.shape[along]
        ends.append(at)
    both = jnp.concatenate(arrays, axis=along)
    return tuple(jnp.split(lax.all_gather(both, axis, axis=dim, tiled=True), ends, axis=along))


def split_hidden(gate, up, modality):
    gate_f = gate.astype(jnp.float32)
    up_f = up.astype(jnp.float32)
    sig = jax.nn.sigmoid(gate_f)
    act = gate_f * sig
    hidden = (act * up_f).astype(jnp.bfloat16)
    image = (modality == 1)[:, None]
    zero = jnp.zeros_like(hidden)
    return (jnp.where(image, zero, hidden), jnp.where(image, hidden, zero), gate_f, up_f, sig, act)


def forward_term(left_text, left_image, right_text, right_image):
    contract = (((1,), (1,)), ((), ()))
    part = lax.dot_general(left_text, right_text, contract, preferred_element_type=jnp.float32)
    return part + lax.dot_general(
        left_image, right_image, contract, preferred_element_type=jnp.float32
    )


def backward_term(left_text, left_image, right_text, right_image):
    part = jnp.dot(left_text, right_text, preferred_element_type=jnp.float32)
    return part + jnp.dot(left_image, right_image, preferred_element_type=jnp.float32)


def per_device(
    ref_gate,
    ref_up,
    ref_residual,
    ref_modality,
    ref_down_text,
    ref_down_image,
    pol_gate,
    pol_up,
    pol_modality,
    pol_segment,
    pair_margin,
    token_cotangent,
    pol_down_text,
    pol_down_image,
):
    ref_text, ref_image, _, _, _, _ = split_hidden(ref_gate, ref_up, ref_modality)
    pol_text, pol_image, gate_f, up_f, sig, act = split_hidden(pol_gate, pol_up, pol_modality)
    seg_ids = jnp.arange(2 * pair_margin.shape[0], dtype=jnp.int32)
    pair_weight = dpo_beta * jax.nn.sigmoid(-dpo_beta * pair_margin)
    table = jnp.repeat(pair_weight, 2) * jnp.where(seg_ids % 2 == 0, -1.0, 1.0).astype(jnp.float32)
    coef = jnp.sum(
        jnp.where(pol_segment[:, None] == seg_ids[None, :], table[None, :], jnp.float32(0.0)),
        axis=1,
    )
    local_cot = (coef[:, None] * token_cotangent.astype(jnp.float32)).astype(jnp.bfloat16)
    full_cot = lax.all_gather(local_cot, "tp", axis=1, tiled=True)
    image_p = (pol_modality == 1)[:, None]
    zero_cot = jnp.zeros_like(full_cot)
    cot_text = jnp.where(image_p, zero_cot, full_cot)
    cot_image = jnp.where(image_p, full_cot, zero_cot)
    whole_rt, whole_ri, whole_pt, whole_pi = sent_together(
        (ref_down_text, ref_down_image, pol_down_text, pol_down_image), "fsdp", 0, 1
    )
    terms = forward_term(ref_text, ref_image, whole_rt, whole_ri)
    d_hidden = backward_term(cot_text, cot_image, whole_pt, whole_pi)
    summed = lax.psum_scatter(
        terms.astype(jnp.bfloat16), "tp", scatter_dimension=1, tiled=True
    ).astype(jnp.float32)
    ref_out = (summed + ref_residual.astype(jnp.float32)).astype(jnp.bfloat16)
    grad_gate = (d_hidden * up_f * sig * (1.0 + gate_f * (1.0 - sig))).astype(jnp.bfloat16)
    grad_up = (d_hidden * act).astype(jnp.bfloat16)
    width = pol_down_text.shape[1]
    over_rows = (((0,), (0,)), ((), ()))
    term_text = lax.dot_general(cot_text, pol_text, over_rows, preferred_element_type=jnp.float32)
    term_image = lax.dot_general(
        cot_image, pol_image, over_rows, preferred_element_type=jnp.float32
    )
    grads = lax.psum_scatter(
        jnp.concatenate([term_text, term_image], axis=1).astype(jnp.bfloat16),
        "fsdp",
        scatter_dimension=0,
        tiled=True,
    ).astype(jnp.float32)
    return (ref_out, grad_gate, grad_up, grads[:, :width], grads[:, width:])


def solution(mesh):
    in_specs = (
        P("fsdp", "tp"),
        P("fsdp", "tp"),
        P("fsdp", "tp"),
        P("fsdp"),
        P("fsdp", "tp"),
        P("fsdp", "tp"),
        P("fsdp", "tp"),
        P("fsdp", "tp"),
        P("fsdp"),
        P("fsdp"),
        P(),
        P("fsdp", "tp"),
        P("fsdp", "tp"),
        P("fsdp", "tp"),
    )
    out_specs = (
        P("fsdp", "tp"),
        P("fsdp", "tp"),
        P("fsdp", "tp"),
        P("fsdp", "tp"),
        P("fsdp", "tp"),
    )
    return jax.shard_map(
        per_device, mesh=mesh, in_specs=in_specs, out_specs=out_specs, check_vma=False
    )
```

profile of v0, /device:TPU:0, one launch (start us, length us, event | category | flops | bytes accessed | tf_op | source)
XLA Modules:
  0.0 529.0 jit_solution(288210245870872746)
XLA Ops:
  7.2 0.7 divide_multiply_fusion
  7.9 0.1 broadcast_in_dim.66
  7.9 0.1 reshape.33
  8.0 0.8 select_reduce_fusion
  8.8 1.9 multiply_convert_fusion.1
  10.8 0.0 all-gather.3.cloned.1.call-start
  10.8 3.0 pad_maximum_fusion.1
  13.9 0.0 reduce-scatter.5.cloned.1.call-start
  13.9 0.6 copy-done.1
  14.5 67.7 %all-gather.5.cloned.1.call-done = bf16[768,4096]{1,0:T(8,128)(2,1)} async-done(((bf16[768,256]{1,0:T(8,128)(2,1)}), bf16[768,4096]{1,0:T(8,128)(2,1)}) %all-gather.5.cloned.1.call-update) | async-done | bytes 6291472 | tf_op jit(solution)/shard_map/all_gather | solution.py:68
  82.2 8.2 %convolution_convert_fusion = bf16[4096,688]{0,1:T(8,128)(2,1)S(1)} fusion(bf16[768,4096]{1,0:T(8,128)(2,1)} %all-gather.5.cloned.1.call-done, pred[768]{0:T(1024)(128)(4,1)S(1)} %broadcast_compare_fusion, bf16[768,688]{0,1:T(8,128)(2,1)S(1)} %copy-done.6, bf16[768,688]{0,1:T(8,128)(2,1)S(1)} %copy-done.7), kind=kOutput, calls=%fused_computation.2 | convolution fusion | flops 4339240960 | bytes 14041856 | tf_op jit(solution)/shard_map/dot_general | solution.py:87
  90.4 5.3 %convolution_convert_fusion.1 = bf16[4096,688]{0,1:T(8,128)(2,1)S(1)} fusion(bf16[768,4096]{1,0:T(8,128)(2,1)S(1)} %copy-done.3, pred[768]{0:T(1024)(128)(4,1)S(1)} %broadcast_compare_fusion, bf16[768,688]{0,1:T(8,128)(2,1)S(1)} %copy-done.6, bf16[768,688]{0,1:T(8,128)(2,1)S(1)} %copy-done.7), kind=kOutput, calls=%fused_computation.3 | convolution fusion | flops 4339240960 | bytes 14041856 | tf_op jit(solution)/shard_map/dot_general | solution.py:86
  95.7 10.4 %pad_maximum_fusion = bf16[4096,1376]{0,1:T(8,128)(2,1)} fusion(bf16[4096,688]{0,1:T(8,128)(2,1)S(1)} %convolution_convert_fusion, bf16[4096,688]{0,1:T(8,128)(2,1)S(1)} %convolution_convert_fusion.1), kind=kLoop, calls=%fused_computation.1 | loop fusion | flops 22544384 | bytes 22544384 | tf_op jit(solution)/shard_map/concatenate | solution.py:91
  106.2 0.2 reduce-scatter.3.cloned.1.call-start
  106.4 0.4 copy-done.2
  106.8 200.0 %all-gather.3.cloned.1.call-done = bf16[4096,2752]{0,1:T(8,128)(2,1)} async-done(((bf16[512,2752]{0,1:T(8,128)(2,1)}), bf16[4096,2752]{0,1:T(8,128)(2,1)}) %all-gather.3.cloned.1.call-update) | async-done | bytes 22544400 | tf_op jit(solution)/shard_map/all_gather | solution.py:15
  306.8 7.6 %fusion.5 = f32[768,4096]{1,0:T(8,128)S(1)} fusion(bf16[4096,2752]{0,1:T(8,128)(2,1)} %all-gather.3.cloned.1.call-done, pred[768]{0:T(1024)(128)(4,1)S(1)} %broadcast_compare_fusion.1, bf16[768,688]{0,1:T(8,128)(2,1)S(1)} %copy-done.4, bf16[768,688]{0,1:T(8,128)(2,1)S(1)} %copy-done.5), kind=kOutput, calls=%fused_computation.11 | convolution fusion | flops 4333277184 | bytes 20333312 | tf_op jit(solution)/shard_map/dot_general | solution.py:31
  314.4 10.6 %add_convert_fusion = bf16[768,4096]{1,0:T(8,128)(2,1)} fusion(f32[768,4096]{1,0:T(8,128)S(1)} %fusion.5, bf16[4096,2752]{0,1:T(8,128)(2,1)} %all-gather.3.cloned.1.call-done, pred[768]{0:T(1024)(128)(4,1)S(1)} %broadcast_compare_fusion.1, bf16[768,688]{0,1:T(8,128)(2,1)S(1)} %copy-done.4, bf16[768,688]{0,1:T(8,128)(2,1)S(1)} %copy-done.5), kind=kOutput, calls=%fused_computation | convolution fusion | flops 4339568640 | bytes 26624768 | tf_op jit(solution)/shard_map/dot_general | solution.py:32
  325.1 102.9 %reduce-scatter.5.cloned.1.call-done = bf16[512,1376]{0,1:T(8,128)(2,1)} async-done(((bf16[4096,1376]{0,1:T(8,128)(2,1)}), bf16[512,1376]{0,1:T(8,128)(2,1)}) %reduce-scatter.5.cloned.1.call-update) | async-done | bytes 1409040 | tf_op jit(solution)/shard_map/reduce_scatter | solution.py:90
  428.0 3.4 fusion.46
  431.4 8.8 %fusion = f32[768,688]{0,1:T(8,128)S(1)} fusion(bf16[4096,2752]{0,1:T(8,128)(2,1)} %all-gather.3.cloned.1.call-done, bf16[768,4096]{1,0:T(8,128)(2,1)} %all-gather.5.cloned.1.call-done, pred[768]{0:T(1024)(128)(4,1)S(1)} %broadcast_compare_fusion), kind=kOutput, calls=%fused_computation.6 | convolution fusion | flops 4331667456 | bytes 14041856 | tf_op jit(solution)/shard_map/dot_general | solution.py:39
  440.3 9.8 %multiply_convert_fusion = (bf16[768,688]{0,1:T(8,128)(2,1)}, bf16[768,688]{0,1:T(8,128)(2,1)}) fusion(bf16[768,688]{0,1:T(8,128)(2,1)S(1)} %copy-done.8, bf16[768,688]{0,1:T(8,128)(2,1)S(1)} %copy-done.6, f32[768,688]{0,1:T(8,128)S(1)} %fusion, bf16[4096,2752]{0,1:T(8,128)(2,1)} %all-gather.3.cloned.1.call-done, bf16[768,4096]{1,0:T(8,128)(2,1)S(1)} %bitcast.1, ...), kind=kOutput, calls=%fused_computation.33 | convolution fusion | flops 4340121600 | bytes 18268928 | tf_op jit(solution)/shard_map/dot_general | solution.py:38
  450.0 70.6 %reduce-scatter.3.cloned.1.call-done = bf16[768,256]{1,0:T(8,128)(2,1)} async-done(((bf16[768,4096]{1,0:T(8,128)(2,1)}), bf16[768,256]{1,0:T(8,128)(2,1)}) %reduce-scatter.3.cloned.1.call-update) | async-done | bytes 393232 | tf_op jit(solution)/shard_map/reduce_scatter | solution.py:78
  520.6 1.8 add_convert_fusion.1
  (29 shorter events, 0.2 us)
Async XLA Ops:
  7.2 75.0 %all-gather.5.cloned.1.call-start = ((), (), s32[]{:S(2)}) async-start(), calls=%async_computation.4 | async-start | bytes 6684672 | tf_op jit(solution)/shard_map/all_gather | solution.py:68
  10.8 296.1 %all-gather.3.cloned.1.call-start = ((), (), s32[]{:S(2)}) async-start(), calls=%async_computation.2 | async-start | bytes 25362432 | tf_op jit(solution)/shard_map/all_gather | solution.py:15
  13.8 0.7 copy-start.1
  13.8 68.4 %copy-start.6 = (bf16[768,688]{0,1:T(8,128)(2,1)S(1)}, bf16[768,688]{0,1:T(8,128)(2,1)}, u32[]{:S(2)}) copy-start(bf16[768,688]{0,1:T(8,128)(2,1)} %param.21) | copy-start | bytes 3170308
  13.8 68.4 %copy-start.7 = (bf16[768,688]{0,1:T(8,128)(2,1)S(1)}, bf16[768,688]{0,1:T(8,128)(2,1)}, u32[]{:S(2)}) copy-start(bf16[768,688]{0,1:T(8,128)(2,1)} %param.20) | copy-start | bytes 3170308
  13.9 414.1 %reduce-scatter.5.cloned.1.call-start = ((), (), s32[]{:S(2)}) async-start(), calls=%async_computation.5 | async-start | bytes 12681216 | tf_op jit(solution)/shard_map/reduce_scatter | solution.py:90
  82.2 8.2 %copy-start.3 = (bf16[768,4096]{1,0:T(8,128)(2,1)S(1)}, bf16[768,4096]{1,0:T(8,128)(2,1)}, u32[]{:S(2)}) copy-start(bf16[768,4096]{1,0:T(8,128)(2,1)} %all-gather.5.cloned.1.call-done) | copy-start | bytes 18874372
  106.1 0.7 copy-start.2
  106.1 200.7 %copy-start.4 = (bf16[768,688]{0,1:T(8,128)(2,1)S(1)}, bf16[768,688]{0,1:T(8,128)(2,1)}, u32[]{:S(2)}) copy-start(bf16[768,688]{0,1:T(8,128)(2,1)} %param.15) | copy-start | bytes 3170308
  106.2 200.7 %copy-start.5 = (bf16[768,688]{0,1:T(8,128)(2,1)S(1)}, bf16[768,688]{0,1:T(8,128)(2,1)}, u32[]{:S(2)}) copy-start(bf16[768,688]{0,1:T(8,128)(2,1)} %param.14) | copy-start | bytes 3170308
  106.2 414.4 %reduce-scatter.3.cloned.1.call-start = ((), (), s32[]{:S(2)}) async-start(), calls=%async_computation.3 | async-start | bytes 6684672 | tf_op jit(solution)/shard_map/reduce_scatter | solution.py:78
  428.0 12.2 %slice-start = ((s8[6291456]{0:T(1024)(128)(4,1)}), s8[4194304]{0:T(1024)(128)(4,1)S(1)}, s32[]{:S(2)}) async-start(s8[6291456]{0:T(1024)(128)(4,1)} %bitcast), calls=%async_computation.6 | async-start | bytes 8388608
  431.4 8.8 %slice-start.1 = ((s8[6291456]{0:T(1024)(128)(4,1)}), s8[2097152]{0:T(1024)(128)(4,1)S(1)}, s32[]{:S(2)}) async-start(s8[6291456]{0:T(1024)(128)(4,1)} %bitcast), calls=%async_computation.7 | async-start | bytes 4194304
  431.4 8.8 %copy-start.8 = (bf16[768,688]{0,1:T(8,128)(2,1)S(1)}, bf16[768,688]{0,1:T(8,128)(2,1)}, u32[]{:S(2)}) copy-start(bf16[768,688]{0,1:T(8,128)(2,1)} %param.20) | copy-start | bytes 3170308
  440.2 80.4 %copy-start = (bf16[768,256]{1,0:T(8,128)(2,1)S(1)}, bf16[768,256]{1,0:T(8,128)(2,1)}, u32[]{:S(2)}) copy-start(bf16[768,256]{1,0:T(8,128)(2,1)} %param.16) | copy-start | bytes 1179652
Sparse Core Ops, SparseCore 0:
  10.9 71.2 all-gather.4
  83.9 222.9 all-gather.2
  309.2 118.6 reduce-scatter.4
  432.0 88.5 reduce-scatter.2
where the time goes:
time: 529 us
  waiting for transfers between devices  441 us (83%)
  matrix products  50.3 us (10%)
  other arithmetic  18.6 us (4%)
  between operations  13.9 us (3%)
    all_gather x1, waiting for transfers between devices, sent_together(): lax.all_gather(both, axis, axis=dim, tiled=True)  200 us
    reduce_scatter x1, waiting for transfers between devices, per_device(): lax.psum_scatter(jnp.concatenate([term_text, term_image], axis=1).astype(...  103 us
    reduce_scatter x1, waiting for transfers between devices, per_device(): lax.psum_scatter(terms.astype(jnp.bfloat16), 'tp', scatter_dimension=1, t...  70.6 us
    all_gather x1, waiting for transfers between devices, per_device(): full_cot = lax.all_gather(local_cot, 'tp', axis=1, tiled=True)  67.7 us
    dot_general x1, matrix products, forward_term(): lax.dot_general(left_image, right_image, contract, preferred_element_type...  10.6 us
  transfers between devices with their start and end apart: 4, of which 4 were waited for; matrix products, arithmetic and copies ran while one was open for 13% of the time, Pallas kernels for 0%

commit v1 on v0

--- a/solution.py
+++ b/solution.py
@@ -4,6 +4,13 @@
 from jax.sharding import PartitionSpec as P
 
 dpo_beta = 0.1
+
+
+def exchange_gather(x, mesh_axis, dim):
+    n_dev = lax.axis_size(mesh_axis)
+    blocks = jnp.stack([x for _ in range(n_dev)])
+    blocks = lax.all_to_all(blocks, mesh_axis, split_axis=0, concat_axis=0)
+    return jnp.concatenate(blocks, axis=dim)
 
 
 def sent_together(arrays, axis, dim, along):
@@ -65,7 +72,7 @@
         axis=1,
     )
     local_cot = (coef[:, None] * token_cotangent.astype(jnp.float32)).astype(jnp.bfloat16)
-    full_cot = lax.all_gather(local_cot, "tp", axis=1, tiled=True)
+    full_cot = exchange_gather(local_cot, "tp", 1)
     image_p = (pol_modality == 1)[:, None]
     zero_cot = jnp.zeros_like(full_cot)
     cot_text = jnp.where(image_p, zero_cot, full_cot)

time: 529 us -> 565 us (1.068)
  local copies, waits for them, and re-layouts: 4.63 us -> 17.5 us
  waiting for transfers between devices: 441 us -> 452 us
  starting transfers between devices: 0.34 us -> 8.48 us
    all_to_all x0 -> x1, waiting for transfers between devices: none -> 283 us  [exchange_gather(): blocks = lax.all_to_all(blocks, mesh_axis, split_axis=0, concat_axis=0)]
    all_gather x1, waiting for transfers between devices: 200 us -> 0.01 us  [sent_together(): lax.all_gather(both, axis, axis=dim, tiled=True)]
    all_gather x1 -> x0, waiting for transfers between devices: 67.7 us -> none  [per_device(): full_cot = lax.all_gather(local_cot, 'tp', axis=1, tiled=True)]
    all_to_all x0 -> x1, local copies, waits for them, and re-layouts: none -> 8.67 us  [exchange_gather(): blocks = lax.all_to_all(blocks, mesh_axis, split_axis=0, concat_axis=0)]
    all_to_all x0 -> x1, starting transfers between devices: none -> 8.18 us  [exchange_gather(): blocks = lax.all_to_all(blocks, mesh_axis, split_axis=0, concat_axis=0)]
    select_n x0 -> x1, other arithmetic: none -> 6.19 us  [per_device(): cot_text = jnp.where(image_p, zero_cot, full_cot)]
  transfers between devices with their start and end apart: 4 -> 4, of which waited for: 4 -> 3; matrix products, arithmetic and copies ran while one was open for 13% -> 15% of each run, Pallas kernels for 0% -> 0%
where the time goes in v1:
time: 565 us
  waiting for transfers between devices  452 us (80%)
  matrix products  51.4 us (9%)
  other arithmetic  21.5 us (4%)
  local copies, waits for them, and re-layouts  17.5 us (3%)
  between operations  13.9 us (2%)
  starting transfers between devices  8.48 us (2%)
    all_to_all x1, waiting for transfers between devices, exchange_gather(): blocks = lax.all_to_all(blocks, mesh_axis, split_axis=0, concat_axis=0)  283 us
    reduce_scatter x1, waiting for transfers between devices, per_device(): lax.psum_scatter(jnp.concatenate([term_text, term_image], axis=1).astype(...  97.6 us
    reduce_scatter x1, waiting for transfers between devices, per_device(): lax.psum_scatter(terms.astype(jnp.bfloat16), 'tp', scatter_dimension=1, t...  71.1 us
  transfers between devices with their start and end apart: 4, of which 3 were waited for; matrix products, arithmetic and copies ran while one was open for 15% of the time, Pallas kernels for 0%

profile of v1, /device:TPU:0, one launch (start us, length us, event | category | flops | bytes accessed | tf_op | source)
XLA Modules:
  0.0 564.7 jit_solution(8516244707783311369)
XLA Ops:
  7.2 3.0 pad_maximum_fusion.1
  10.3 0.6 copy-done.12
  11.2 0.1 copy-done.1
  11.3 0.2 multiply_convert_fusion.1
  11.4 3.2 stack.2
  14.7 8.2 %all-to-all-start = ((bf16[16,768,256]{2,1,0:T(8,128)(2,1)}), bf16[16,768,256]{2,1,0:T(8,128)(2,1)}, u32[]{:S(2)}, u32[]{:S(2)}) async-start(bf16[16,768,256]{2,1,0:T(8,128)(2,1)} %stack.2), calls=%async_computation.1 | async-start | bytes 12582912 | tf_op jit(solution)/shard_map/all_to_all | solution.py:12
  22.9 283.1 %all-to-all-done = bf16[16,768,256]{2,1,0:T(8,128)(2,1)} async-done(((bf16[16,768,256]{2,1,0:T(8,128)(2,1)}), bf16[16,768,256]{2,1,0:T(8,128)(2,1)}, u32[]{:S(2)}, u32[]{:S(2)}) %all-to-all-start) | async-done | bytes 6291488 | tf_op jit(solution)/shard_map/all_to_all | solution.py:12
  306.0 8.7 %copy.20 = bf16[16,768,256]{1,2,0:T(8,128)(2,1)} copy(bf16[16,768,256]{2,1,0:T(8,128)(2,1)} %all-to-all-done) | data formatting | bytes 12582912 | tf_op jit(solution)/shard_map/all_to_all | solution.py:12
  314.7 6.2 %bitcast_select_fusion.1 = (bf16[768,4096]{0,1:T(8,128)(2,1)S(1)}, bf16[768,4096]{0,1:T(8,128)(2,1)}) fusion(bf16[16,768,256]{1,2,0:T(8,128)(2,1)} %copy.20, pred[768]{0:T(1024)(128)(4,1)S(1)} %broadcast_compare_fusion), kind=kLoop, calls=%fused_computation.5 | loop fusion | flops 6291456 | bytes 18875136 | tf_op jit(solution)/shard_map/jit(_where)/select_n | solution.py:78
  320.9 10.3 %convolution_convert_fusion = bf16[4096,688]{0,1:T(8,128)(2,1)S(1)} fusion(bf16[768,4096]{0,1:T(8,128)(2,1)} %get-tuple-element.6, pred[768]{0:T(1024)(128)(4,1)S(1)} %broadcast_compare_fusion, bf16[768,688]{0,1:T(8,128)(2,1)} %param.21, bf16[768,688]{0,1:T(8,128)(2,1)} %param.20), kind=kOutput, calls=%fused_computation.2 | convolution fusion | flops 4336095232 | bytes 14041856 | tf_op jit(solution)/shard_map/dot_general | solution.py:94
  331.2 5.1 convolution_convert_fusion.1
  336.4 10.2 %pad_maximum_fusion = bf16[4096,1376]{0,1:T(8,128)(2,1)} fusion(bf16[4096,688]{0,1:T(8,128)(2,1)S(1)} %convolution_convert_fusion, bf16[4096,688]{0,1:T(8,128)(2,1)S(1)} %convolution_convert_fusion.1), kind=kLoop, calls=%fused_computation.1 | loop fusion | flops 22544384 | bytes 22544384 | tf_op jit(solution)/shard_map/concatenate | solution.py:98
  346.6 0.2 reduce-scatter.3.cloned.1.call-start
  346.8 0.4 copy-done.4
  347.2 0.5 copy-done.6
  347.8 0.3 copy-done.7
  348.1 7.6 %fusion.5 = f32[768,4096]{1,0:T(8,128)S(1)} fusion(bf16[4096,2752]{0,1:T(8,128)(2,1)} %all-gather.2.cloned.1.call-done, pred[768]{0:T(1024)(128)(4,1)S(1)} %broadcast_compare_fusion.1, bf16[768,688]{0,1:T(8,128)(2,1)S(1)} %copy-done.6, bf16[768,688]{0,1:T(8,128)(2,1)S(1)} %copy-done.7), kind=kOutput, calls=%fused_computation.11 | convolution fusion | flops 4333277184 | bytes 20333312 | tf_op jit(solution)/shard_map/dot_general | solution.py:38
  355.7 10.2 %add_convert_fusion = bf16[768,4096]{1,0:T(8,128)(2,1)} fusion(f32[768,4096]{1,0:T(8,128)S(1)} %fusion.5, bf16[4096,2752]{0,1:T(8,128)(2,1)} %all-gather.2.cloned.1.call-done, pred[768]{0:T(1024)(128)(4,1)S(1)} %broadcast_compare_fusion.1, bf16[768,688]{0,1:T(8,128)(2,1)S(1)} %copy-done.6, bf16[768,688]{0,1:T(8,128)(2,1)S(1)} %copy-done.7), kind=kOutput, calls=%fused_computation | convolution fusion | flops 4339568640 | bytes 26624768 | tf_op jit(solution)/shard_map/dot_general | solution.py:39
  365.9 97.6 %reduce-scatter.5.cloned.1.call-done = bf16[512,1376]{0,1:T(8,128)(2,1)} async-done(((bf16[4096,1376]{0,1:T(8,128)(2,1)}), bf16[512,1376]{0,1:T(8,128)(2,1)}) %reduce-scatter.5.cloned.1.call-update) | async-done | bytes 1409040 | tf_op jit(solution)/shard_map/reduce_scatter | solution.py:97
  463.5 3.4 fusion.44
  466.9 8.5 %fusion = f32[768,688]{0,1:T(8,128)S(1)} fusion(bf16[768,4096]{0,1:T(8,128)(2,1)} %get-tuple-element.6, bf16[4096,2752]{0,1:T(8,128)(2,1)} %all-gather.2.cloned.1.call-done), kind=kOutput, calls=%fused_computation.6 | convolution fusion | flops 4328521728 | bytes 14041088 | tf_op jit(solution)/shard_map/dot_general | solution.py:46
  475.5 9.7 %multiply_convert_fusion = (bf16[768,688]{0,1:T(8,128)(2,1)}, bf16[768,688]{0,1:T(8,128)(2,1)}) fusion(bf16[768,688]{0,1:T(8,128)(2,1)S(1)} %copy-done.11, bf16[768,688]{0,1:T(8,128)(2,1)S(1)} %copy-done.9, f32[768,688]{0,1:T(8,128)S(1)} %fusion, bf16[768,4096]{0,1:T(8,128)(2,1)S(1)} %bitcast.10, bf16[4096,2752]{0,1:T(8,128)(2,1)} %all-gather.2.cloned.1.call-done), kind=kOutput, calls=%fused_computation.33 | convolution fusion | flops 4336975872 | bytes 18268160 | tf_op jit(solution)/shard_map/dot_general | solution.py:45
  485.2 71.1 %reduce-scatter.3.cloned.1.call-done = bf16[768,256]{1,0:T(8,128)(2,1)} async-done(((bf16[768,4096]{1,0:T(8,128)(2,1)}), bf16[768,256]{1,0:T(8,128)(2,1)}) %reduce-scatter.3.cloned.1.call-update) | async-done | bytes 393232 | tf_op jit(solution)/shard_map/reduce_scatter | solution.py:85
  556.3 1.8 add_convert_fusion.1
  (39 shorter events, 0.4 us)
Async XLA Ops:
  7.2 340.1 %all-gather.2.cloned.1.call-start = ((), (), s32[]{:S(2)}) async-start(), calls=%async_computation.3 | async-start | bytes 25362432 | tf_op jit(solution)/shard_map/all_gather | solution.py:22
  10.2 0.7 copy-start.12
  10.2 0.8 copy-start.5
  10.2 1.0 copy-start.1
  14.7 8.2 %copy-start.3 = (s32[768]{0:T(1024)S(1)}, s32[768]{0:T(1024)}, u32[]{:S(2)}) copy-start(s32[768]{0:T(1024)} %param.22) | copy-start | bytes 9220
  14.7 291.3 %all-to-all-start = ((bf16[16,768,256]{2,1,0:T(8,128)(2,1)}), bf16[16,768,256]{2,1,0:T(8,128)(2,1)}, u32[]{:S(2)}, u32[]{:S(2)}) async-start(bf16[16,768,256]{2,1,0:T(8,128)(2,1)} %stack.2), calls=%async_computation.1 | async-start | bytes 12582912 | tf_op jit(solution)/shard_map/all_to_all | solution.py:12
  22.9 440.7 %reduce-scatter.5.cloned.1.call-start = ((), (), s32[]{:S(2)}) async-start(), calls=%async_computation.5 | async-start | bytes 12681216 | tf_op jit(solution)/shard_map/reduce_scatter | solution.py:97
  320.9 10.3 %copy-start = (bf16[768,4096]{0,1:T(8,128)(2,1)}, bf16[768,4096]{0,1:T(8,128)(2,1)S(1)}, u32[]{:S(2)}) copy-start(bf16[768,4096]{0,1:T(8,128)(2,1)S(1)} %get-tuple-element.5) | copy-start | bytes 18874372
  320.9 10.4 %copy-start.8 = (bf16[768,688]{0,1:T(8,128)(2,1)S(1)}, bf16[768,688]{0,1:T(8,128)(2,1)}, u32[]{:S(2)}) copy-start(bf16[768,688]{0,1:T(8,128)(2,1)} %param.21) | copy-start | bytes 3170308
  320.9 10.4 %copy-start.10 = (bf16[768,688]{0,1:T(8,128)(2,1)S(1)}, bf16[768,688]{0,1:T(8,128)(2,1)}, u32[]{:S(2)}) copy-start(bf16[768,688]{0,1:T(8,128)(2,1)} %param.20) | copy-start | bytes 3170308
  346.6 0.7 copy-start.4
  346.6 1.2 copy-start.6
  346.6 1.6 copy-start.7
  346.6 209.7 %reduce-scatter.3.cloned.1.call-start = ((), (), s32[]{:S(2)}) async-start(), calls=%async_computation.4 | async-start | bytes 6684672 | tf_op jit(solution)/shard_map/reduce_scatter | solution.py:85
  463.5 12.0 %slice-start = ((s8[6291456]{0:T(1024)(128)(4,1)}), s8[4194304]{0:T(1024)(128)(4,1)S(1)}, s32[]{:S(2)}) async-start(s8[6291456]{0:T(1024)(128)(4,1)} %bitcast.9), calls=%async_computation.6 | async-start | bytes 8388608
  466.9 8.6 %slice-start.1 = ((s8[6291456]{0:T(1024)(128)(4,1)}), s8[2097152]{0:T(1024)(128)(4,1)S(1)}, s32[]{:S(2)}) async-start(s8[6291456]{0:T(1024)(128)(4,1)} %bitcast.9), calls=%async_computation.7 | async-start | bytes 4194304
  466.9 8.6 %copy-start.9 = (bf16[768,688]{0,1:T(8,128)(2,1)S(1)}, bf16[768,688]{0,1:T(8,128)(2,1)}, u32[]{:S(2)}) copy-start(bf16[768,688]{0,1:T(8,128)(2,1)} %param.21) | copy-start | bytes 3170308
  466.9 8.6 %copy-start.11 = (bf16[768,688]{0,1:T(8,128)(2,1)S(1)}, bf16[768,688]{0,1:T(8,128)(2,1)}, u32[]{:S(2)}) copy-start(bf16[768,688]{0,1:T(8,128)(2,1)} %param.20) | copy-start | bytes 3170308
  475.5 80.8 %copy-start.2 = (bf16[768,256]{1,0:T(8,128)(2,1)S(1)}, bf16[768,256]{1,0:T(8,128)(2,1)}, u32[]{:S(2)}) copy-start(bf16[768,256]{1,0:T(8,128)(2,1)} %param.16) | copy-start | bytes 1179652
Sparse Core Ops, SparseCore 0:
  10.4 277.7 all-gather.1
  346.7 116.7 reduce-scatter.4
  467.7 88.5 reduce-scatter.2
